TPU v7x, 16 devices: a 4x2x1 block of a 4x4x8 slice. The times are simulated.
16 devices in a mesh: data: 2 (over y, z), model: 8 (over x, core).
Axes of the slice: x: 4, y: 2, z: 1, core: 2. Of those that a mesh axis runs over, the one named last changes fastest.
The devices are a block of a 4x4x8 slice.
Arguments:
- hidden_in: bfloat16 [256, 1024], P('data'), parts along dimension 0
- positions: int32 [256], P('data'), parts along dimension 0
- norm_attn: bfloat16 [4, 1024], replicated
- norm_mlp: bfloat16 [4, 1024], replicated
- w_query: bfloat16 [4, 1024, 1024], P(None, None, 'model')
- w_key: bfloat16 [4, 1024, 1024], P(None, None, 'model')
- w_value: bfloat16 [4, 1024, 1024], P(None, None, 'model')
- w_out: bfloat16 [4, 1024, 1024], P(None, 'model')
- w_gate: bfloat16 [4, 1024, 2816], P(None, None, 'model')
- w_up: bfloat16 [4, 1024, 2816], P(None, None, 'model')
- w_down: bfloat16 [4, 2816, 1024], P(None, 'model')
- key_cache: bfloat16 [4, 256, 128, 16, 64], P(None, 'data', None, 'model'), parts along dimension 1
- value_cache: bfloat16 [4, 256, 128, 16, 64], P(None, 'data', None, 'model'), parts along dimension 1
Outputs:
- output 1: bfloat16 [256, 1024], P('data'), parts along dimension 0
- output 2: bfloat16 [4, 256, 128, 16, 64], P(None, 'data', None, 'model'), parts along dimension 1
- output 3: bfloat16 [4, 256, 128, 16, 64], P(None, 'data', None, 'model'), parts along dimension 1
There are 2 independent parts. A program takes and returns all parts, laid end to end along the dimension named above; an argument that names none is the same for every part.
All inputs are finite; a program needn't handle non-finite values.
Results may differ from a plain program's by a relative error of at most 0.02.
Values are sent between devices in bfloat16 or wider.
A program may use at most 768 MiB of HBM per device.

v0:
```python
import jax
import jax.numpy as jnp
from jax import lax
from jax.sharding import PartitionSpec as P

NORM_EPS = 1e-6
ROPE_BASE = 10000.0


def rms_norm(vals, gain):
    vals_f = vals.astype(jnp.float32)
    inv_rms = lax.rsqrt(jnp.mean(vals_f * vals_f, axis=-1, keepdims=True) + NORM_EPS)
    return (vals_f * inv_rms * gain.astype(jnp.float32)).astype(jnp.bfloat16)


def rope_tables(positions, head_dim):
    half = head_dim // 2
    inv_freq = ROPE_BASE ** (-jnp.arange(half, dtype=jnp.float32) / half)
    angles = positions.astype(jnp.float32)[:, None] * inv_freq[None, :]
    return jnp.cos(angles), jnp.sin(angles)


def apply_rope(vals, cos_tab, sin_tab):
    half = vals.shape[-1] // 2
    vals_f = vals.astype(jnp.float32)
    first = vals_f[..., :half]
    second = vals_f[..., half:]
    cos_b = cos_tab[:, None, :]
    sin_b = sin_tab[:, None, :]
    return jnp.concatenate([first * cos_b - second * sin_b, second * cos_b + first * sin_b], axis=-1).astype(jnp.bfloat16)


def attention(hidden, positions, cos_tab, sin_tab, q_proj, k_proj, v_proj, k_cache, v_cache):
    batch = hidden.shape[0]
    cache_len = k_cache.shape[1]
    kv_heads = k_cache.shape[2]
    head_dim = k_cache.shape[3]
    q_heads = q_proj.shape[1] // head_dim
    group = q_heads // kv_heads
    query = jnp.dot(hidden, q_proj, preferred_element_type=jnp.float32).astype(jnp.bfloat16).reshape(batch, q_heads, head_dim)
    key_new = jnp.dot(hidden, k_proj, preferred_element_type=jnp.float32).astype(jnp.bfloat16).reshape(batch, kv_heads, head_dim)
    value_new = jnp.dot(hidden, v_proj, preferred_element_type=jnp.float32).astype(jnp.bfloat16).reshape(batch, kv_heads, head_dim)
    query = apply_rope(query, cos_tab, sin_tab)
    key_new = apply_rope(key_new, cos_tab, sin_tab)
    slots = jnp.arange(cache_len)
    write_row = (slots[None, :] == positions[:, None])[:, :, None, None]
    k_cache = jnp.where(write_row, key_new[:, None], k_cache)
    v_cache = jnp.where(write_row, value_new[:, None], v_cache)
    query_g = query.reshape(batch, kv_heads, group, head_dim)
    scores = jnp.einsum("bkgd,bskd->bkgs", query_g, k_cache, preferred_element_type=jnp.float32) * (head_dim ** -0.5)
    visible = (slots[None, :] <= positions[:, None])[:, None, None, :]
    scores = jnp.where(visible, scores, -1e30)
    attn_prob = jax.nn.softmax(scores, axis=-1).astype(jnp.bfloat16)
    attn_val = jnp.einsum("bkgs,bskd->bkgd", attn_prob, v_cache, preferred_element_type=jnp.float32).astype(jnp.bfloat16)
    return attn_val.reshape(batch, q_heads * head_dim), k_cache, v_cache


def gated_mlp(hidden, gate_proj, up_proj):
    gate_pre = jnp.dot(hidden, gate_proj, preferred_element_type=jnp.float32)
    up_val = jnp.dot(hidden, up_proj, preferred_element_type=jnp.float32)
    return (jax.nn.silu(gate_pre) * up_val).astype(jnp.bfloat16)


def add_residual(residual, delta):
    return (residual.astype(jnp.float32) + delta.astype(jnp.float32)).astype(jnp.bfloat16)


def solution(mesh):
    def local_step(hidden_in, positions, norm_attn, norm_mlp, w_query, w_key, w_value, w_out, w_gate, w_up, w_down, key_cache, value_cache):
        cos_tab, sin_tab = rope_tables(positions, key_cache.shape[-1])
        residual = hidden_in
        key_list = []
        value_list = []
        for layer in range(key_cache.shape[0]):
            hidden = rms_norm(residual, norm_attn[layer])
            attn_val, kc_new, vc_new = attention(hidden, positions, cos_tab, sin_tab, w_query[layer], w_key[layer], w_value[layer], key_cache[layer], value_cache[layer])
            key_list.append(kc_new)
            value_list.append(vc_new)
            attn_part = jnp.dot(attn_val, w_out[layer], preferred_element_type=jnp.float32).astype(jnp.bfloat16)
            residual = add_residual(residual, lax.psum(attn_part, "model"))
            hidden = rms_norm(residual, norm_mlp[layer])
            act_val = gated_mlp(hidden, w_gate[layer], w_up[layer])
            mlp_part = jnp.dot(act_val, w_down[layer], preferred_element_type=jnp.float32).astype(jnp.bfloat16)
            residual = add_residual(residual, lax.psum(mlp_part, "model"))
        return residual, jnp.stack(key_list), jnp.stack(value_list)

    row_spec = P("data", None)
    col_spec = P(None, None, "model")
    split_spec = P(None, "model", None)
    cache_spec = P(None, "data", None, "model", None)
    in_specs = (row_spec, P("data"), P(None, None), P(None, None), col_spec, col_spec, col_spec, split_spec, col_spec, col_spec, split_spec, cache_spec, cache_spec)
    out_specs = (row_spec, cache_spec, cache_spec)
    return jax.shard_map(local_step, mesh=mesh, in_specs=in_specs, out_specs=out_specs, check_vma=False)
```

profile of v0, /device:TPU:113, one launch (start us, length us, event | category | flops | bytes accessed | tf_op | source)
XLA Modules:
  0.0 515.8 jit_solution(17530537623056052911)
XLA Ops:
  8.7 1.1 fusion.100
  10.6 1.3 convolution_convert_fusion.18
  12.0 1.3 convolution_convert_fusion.17
  13.3 1.4 convolution_convert_fusion.19
  15.3 4.5 fusion.15
  20.1 4.6 fusion.14
  26.0 52.8 %all-reduce.9.cloned.1.call-done = bf16[128,1024]{1,0:T(8,128)(2,1)} async-done(((bf16[128,1024]{1,0:T(8,128)(2,1)}), bf16[128,1024]{1,0:T(8,128)(2,1)}) %all-reduce.9.cloned.1.call-update) | async-done | bytes 262160 | tf_op jit(solution)/shard_map/psum | solution.py:80
  78.8 1.1 fusion.104
  79.9 1.5 fusion.82
  81.5 3.0 convolution_convert_fusion.6
  84.7 51.0 %all-reduce.11.cloned.1.call-done = bf16[128,1024]{1,0:T(8,128)(2,1)} async-done(((bf16[128,1024]{1,0:T(8,128)(2,1)}), bf16[128,1024]{1,0:T(8,128)(2,1)}) %all-reduce.11.cloned.1.call-update) | async-done | bytes 262160 | tf_op jit(solution)/shard_map/psum | solution.py:84
  135.7 1.1 fusion.108
  136.8 1.1 fusion.110
  138.2 1.2 convolution_convert_fusion.15
  139.4 1.2 convolution_convert_fusion.16
  141.1 4.5 fusion.13
  145.9 4.6 fusion.12
  151.7 51.0 %all-reduce.13.cloned.1.call-done = bf16[128,1024]{1,0:T(8,128)(2,1)} async-done(((bf16[128,1024]{1,0:T(8,128)(2,1)}), bf16[128,1024]{1,0:T(8,128)(2,1)}) %all-reduce.13.cloned.1.call-update) | async-done | bytes 262160 | tf_op jit(solution)/shard_map/psum | solution.py:80
  202.7 1.2 fusion.112
  203.9 1.5 fusion.77
  205.4 3.0 convolution_convert_fusion.4
  208.7 50.8 %all-reduce.15.cloned.1.call-done = bf16[128,1024]{1,0:T(8,128)(2,1)} async-done(((bf16[128,1024]{1,0:T(8,128)(2,1)}), bf16[128,1024]{1,0:T(8,128)(2,1)}) %all-reduce.15.cloned.1.call-update) | async-done | bytes 262160 | tf_op jit(solution)/shard_map/psum | solution.py:84
  259.6 1.1 fusion.116
  260.7 1.1 fusion.118
  262.0 1.2 convolution_convert_fusion.12
  263.3 1.2 convolution_convert_fusion.13
  265.0 4.5 fusion.11
  269.8 4.6 fusion.10
  275.5 51.0 %all-reduce.17.cloned.1.call-done = bf16[128,1024]{1,0:T(8,128)(2,1)} async-done(((bf16[128,1024]{1,0:T(8,128)(2,1)}), bf16[128,1024]{1,0:T(8,128)(2,1)}) %all-reduce.17.cloned.1.call-update) | async-done | bytes 262160 | tf_op jit(solution)/shard_map/psum | solution.py:80
  326.6 1.2 fusion.120
  327.7 1.5 fusion.72
  329.3 3.0 convolution_convert_fusion.2
  332.4 51.0 %all-reduce.19.cloned.1.call-done = bf16[128,1024]{1,0:T(8,128)(2,1)} async-done(((bf16[128,1024]{1,0:T(8,128)(2,1)}), bf16[128,1024]{1,0:T(8,128)(2,1)}) %all-reduce.19.cloned.1.call-update) | async-done | bytes 262160 | tf_op jit(solution)/shard_map/psum | solution.py:84
  383.4 1.1 fusion.124
  384.6 1.1 fusion.126
  385.9 1.2 convolution_convert_fusion.9
  387.1 1.2 convolution_convert_fusion.10
  388.9 4.5 fusion.9
  393.6 4.6 fusion.8
  398.3 1.0 convolution_convert_fusion.1
  399.4 23.5 %broadcast_select_fusion.3 = (bf16[1,128,128,2,64]{2,4,3,1,0:T(8,128)(2,1)}, bf16[1,128,128,2,64]{2,4,3,1,0:T(8,128)(2,1)}, bf16[1,128,128,2,64]{2,4,3,1,0:T(8,1...) fusion(pred[128,128]{1,0:T(8,128)(4,1)S(1)} %get-tuple-element., ...), kind=kLoop, calls=%fused_computation.29 | loop fusion | flops 16777216 | bytes 67387392 | tf_op jit(solution)/shard_map/jit(_where)/select_n | solution.py:48
  422.9 27.5 %all-reduce.21.cloned.1.call-done = bf16[128,1024]{1,0:T(8,128)(2,1)} async-done(((bf16[128,1024]{1,0:T(8,128)(2,1)}), bf16[128,1024]{1,0:T(8,128)(2,1)}) %all-reduce.21.cloned.1.call-update) | async-done | bytes 262160 | tf_op jit(solution)/shard_map/psum | solution.py:80
  450.4 1.2 fusion.128
  451.6 1.5 fusion.67
  453.1 3.0 convolution_convert_fusion
  456.2 23.2 %pad_maximum_fusion = (bf16[4,128,128,2,64]{2,4,3,1,0:T(8,128)(2,1)}, bf16[4,128,128,2,64]{2,4,3,1,0:T(8,128)(2,1)}) fusion(bf16[1,128,128,2,64]{2,4,3,1,0:T(8,128)(2,1)} %get-tuple-element.43, bf16[1,128,128,2,64]{2,4,3,1,0:T(8,128)(2,1)} %get-tuple-element.44, bf16[1,128,128,2,64]{2,4,3,1,0:T(8,128)(2,1)} %get-tuple-element.45, ...), kind=kLoop, calls=%fused_computation.8 | loop fusion | flops 50331648 | bytes 67108864 | tf_op jit(solution)/shard_map/stack | solution.py:85
  479.3 27.9 %all-reduce.23.cloned.1.call-done = bf16[128,1024]{1,0:T(8,128)(2,1)} async-done(((bf16[128,1024]{1,0:T(8,128)(2,1)}), bf16[128,1024]{1,0:T(8,128)(2,1)}) %all-reduce.23.cloned.1.call-update) | async-done | bytes 262160 | tf_op jit(solution)/shard_map/psum | solution.py:84
  507.3 1.7 fusion.131
  (90 shorter events, 10.3 us)
Async XLA Ops:
  7.2 71.6 %all-reduce.9.cloned.1.call-start = ((), (), s32[]{:S(2)}) async-start(), calls=%async_computation | async-start | bytes 524288 | tf_op jit(solution)/shard_map/psum | solution.py:80
  20.1 4.8 copy-start.3
  20.1 5.9 %copy-start.6 = (bf16[4,1024]{1,0:T(4,128)(2,1)S(1)}, bf16[4,1024]{1,0:T(4,128)(2,1)}, u32[]{:S(2)}) copy-start(bf16[4,1024]{1,0:T(4,128)(2,1)} %param.16) | copy-start | bytes 24580
  20.1 58.7 %copy-start.4 = (bf16[128,1024]{1,0:T(8,128)(2,1)S(1)}, bf16[128,1024]{1,0:T(8,128)(2,1)}, u32[]{:S(2)}) copy-start(bf16[128,1024]{1,0:T(8,128)(2,1)} %param.13) | copy-start | bytes 786436
  24.7 113.1 %copy-start.5 = (bf16[4,1024,128]{2,1,0:T(8,128)(2,1)S(1)}, bf16[4,1024,128]{2,1,0:T(8,128)(2,1)}, u32[]{:S(2)}) copy-start(bf16[4,1024,128]{2,1,0:T(8,128)(2,1)} %param.19) | copy-start | bytes 3145732
  25.9 109.8 %all-reduce.11.cloned.1.call-start = ((), (), s32[]{:S(2)}) async-start(), calls=%async_computation.1 | async-start | bytes 524288 | tf_op jit(solution)/shard_map/psum | solution.py:84
  84.6 118.1 %all-reduce.13.cloned.1.call-start = ((), (), s32[]{:S(2)}) async-start(), calls=%async_computation.2 | async-start | bytes 524288 | tf_op jit(solution)/shard_map/psum | solution.py:80
  145.9 56.8 %copy-start.1 = (bf16[128,1024]{1,0:T(8,128)(2,1)S(1)}, bf16[128,1024]{1,0:T(8,128)(2,1)}, u32[]{:S(2)}) copy-start(bf16[128,1024]{1,0:T(8,128)(2,1)} %all-reduce.11.cloned.1.call-done) | copy-start | bytes 786436
  151.6 108.0 %all-reduce.15.cloned.1.call-start = ((), (), s32[]{:S(2)}) async-start(), calls=%async_computation.3 | async-start | bytes 524288 | tf_op jit(solution)/shard_map/psum | solution.py:84
  208.5 118.1 %all-reduce.17.cloned.1.call-start = ((), (), s32[]{:S(2)}) async-start(), calls=%async_computation.4 | async-start | bytes 524288 | tf_op jit(solution)/shard_map/psum | solution.py:80
  269.7 56.8 %copy-start.2 = (bf16[128,1024]{1,0:T(8,128)(2,1)S(1)}, bf16[128,1024]{1,0:T(8,128)(2,1)}, u32[]{:S(2)}) copy-start(bf16[128,1024]{1,0:T(8,128)(2,1)} %all-reduce.15.cloned.1.call-done) | copy-start | bytes 786436
  275.5 108.0 %all-reduce.19.cloned.1.call-start = ((), (), s32[]{:S(2)}) async-start(), calls=%async_computation.5 | async-start | bytes 524288 | tf_op jit(solution)/shard_map/psum | solution.py:84
  332.3 118.1 %all-reduce.21.cloned.1.call-start = ((), (), s32[]{:S(2)}) async-start(), calls=%async_computation.6 | async-start | bytes 524288 | tf_op jit(solution)/shard_map/psum | solution.py:80
  399.3 51.1 %copy-start = (bf16[128,1024]{1,0:T(8,128)(2,1)S(1)}, bf16[128,1024]{1,0:T(8,128)(2,1)}, u32[]{:S(2)}) copy-start(bf16[128,1024]{1,0:T(8,128)(2,1)} %all-reduce.19.cloned.1.call-done) | copy-start | bytes 786436
  399.3 107.9 %all-reduce.23.cloned.1.call-start = ((), (), s32[]{:S(2)}) async-start(), calls=%async_computation.7 | async-start | bytes 524288 | tf_op jit(solution)/shard_map/psum | solution.py:84
Sparse Core Ops, SparseCore 0:
  26.0 52.7 all-reduce.8
  84.7 50.9 all-reduce.10
  151.7 50.9 all-reduce.12
  208.6 50.9 all-reduce.14
  275.6 50.9 all-reduce.16
  332.4 50.9 all-reduce.18
  399.4 50.9 all-reduce.20
  456.3 50.9 all-reduce.22
where the time goes:
time: 520 us; the launch traced here: 516 us
  waiting for transfers between devices  364 us (70%)
  matrix products  70.8 us (14%)
  other arithmetic  64.2 us (12%)
  between operations  14.6 us (3%)
    psum x4, waiting for transfers between devices, local_step(): residual = add_residual(residual, lax.psum(attn_part, 'model'))  182 us
    psum x4, waiting for transfers between devices, local_step(): residual = add_residual(residual, lax.psum(mlp_part, 'model'))  181 us
    select_n x1, other arithmetic, attention(): v_cache = jnp.where(write_row, value_new[:, None], v_cache)  23.5 us
    another operation x1, other arithmetic, local_step(): return (residual, jnp.stack(key_list), jnp.stack(value_list))  23.2 us
    dot_general x4, matrix products, attention(): jnp.einsum('bkgs,bskd->bkgd', attn_prob, v_cache, preferred_element_type=...  18.4 us
    dot_general x4, matrix products, attention(): jnp.einsum('bkgd,bskd->bkgs', query_g, k_cache, preferred_element_type=jn...  18.1 us
    dot_general x4, matrix products, local_step(): jnp.dot(act_val, w_down[layer], preferred_element_type=jnp.float32)  12 us
  transfers between devices with their start and end apart: 8, of which 8 were waited for; matrix products, arithmetic and copies ran while one was open for 9% of the time, Pallas kernels for 0%

commit v1 on v0

v1 whole, which is shorter than its diff:
```python
import functools
import jax
import jax.numpy as jnp
from jax import lax
from jax.experimental import pallas as pl
from jax.experimental.pallas import tpu as pltpu
from jax.sharding import PartitionSpec as P

NORM_EPS = 1e-6
ROPE_BASE = 10000.0
MESH = pl.DeviceIdType.MESH
GROUP = 8
BLOCK = 32
F32 = jnp.float32
BF16 = jnp.bfloat16


def rms_rows(vals_f, gain):
    inv_rms = lax.rsqrt(jnp.mean(vals_f * vals_f, axis=-1, keepdims=True) + NORM_EPS)
    return (vals_f * inv_rms * gain.astype(F32)).astype(BF16)


def rope_tables(positions, head_dim, heads):
    half = head_dim // 2
    inv_freq = ROPE_BASE ** (-jnp.arange(half, dtype=F32) / half)
    angles = positions.astype(F32)[:, None] * inv_freq[None, :]
    cos_tab, sin_tab = jnp.cos(angles), jnp.sin(angles)
    cos_full = jnp.concatenate([cos_tab, cos_tab] * heads, axis=-1)
    sin_full = jnp.concatenate([-sin_tab, sin_tab] * heads, axis=-1)
    return cos_full, sin_full


def attn_kernel(layer, head_dim, scale, first, *refs):
    if first:
        (pos_ref, x_ref, gain_ref, cos_ref, sin_ref, posb_ref, wq_ref, wk_ref, wv_ref, wo_ref, k_ref, v_ref,
         part_ref, ko_ref, vo_ref, q_s, kn_s, vn_s, o_s) = refs
    else:
        (pos_ref, x_ref, gain_ref, cos_ref, sin_ref, posb_ref, wq_ref, wk_ref, wv_ref, wo_ref, k_ref, v_ref, _, _,
         part_ref, ko_ref, vo_ref, q_s, kn_s, vn_s, o_s) = refs
    step = pl.program_id(0)
    tokens, width = q_s.shape[0] // 2, q_s.shape[1]
    half = head_dim // 2
    groups = tokens // GROUP

    def by_head(vals):
        lane = lax.broadcasted_iota(jnp.int32, (groups, GROUP, width), 2)
        vals3 = vals.reshape(groups, GROUP, width)
        low = jnp.where(lane < head_dim, vals3, 0.0)
        high = jnp.where(lane < head_dim, 0.0, vals3)
        return jnp.concatenate([low, high], axis=1).reshape(2 * tokens, width)

    @pl.when(step == 0)
    def _():
        if first:
            hidden = rms_rows(x_ref[...].astype(F32), gain_ref[...])
        else:
            hidden = x_ref[...]
        lane = lax.broadcasted_iota(jnp.int32, (tokens, width), 1)
        lower = lax.rem(lane, head_dim) < half

        def rope(vals):
            turned = jnp.where(lower, pltpu.roll(vals, width - half, 1), pltpu.roll(vals, half, 1))
            return (vals * cos_ref[...] + turned * sin_ref[...]).astype(BF16).astype(F32)

        def project(w_ref):
            return jnp.dot(hidden, w_ref[layer], preferred_element_type=F32).astype(BF16).astype(F32)

        q_s[...] = by_head(rope(project(wq_ref)))
        kn_s[...] = by_head(rope(project(wk_ref)))
        vn_s[...] = by_head(project(wv_ref))

    rows = 2 * GROUP
    row = lax.broadcasted_iota(jnp.int32, (rows, width), 0)
    tok = lax.rem(row, GROUP)
    lane = lax.broadcasted_iota(jnp.int32, (rows, width), 1)
    lane_b = lane.astype(F32).astype(BF16)
    head_low = lax.broadcasted_iota(jnp.int32, (GROUP, width), 1) < head_dim
    per_step = BLOCK // GROUP
    for g in range(per_step):
        base = pl.multiple_of((step * per_step + g) * rows, rows)
        q_f = q_s[pl.ds(base, rows), :]
        kn_f = kn_s[pl.ds(base, rows), :]
        vn_f = vn_s[pl.ds(base, rows), :]
        pos = posb_ref[pl.ds(base, rows), :]
        keys = [k_ref[0, g * GROUP + t] for t in range(GROUP)]
        vals = [v_ref[0, g * GROUP + t] for t in range(GROUP)]
        prod = jnp.dot(q_f.astype(BF16), jnp.concatenate(keys, axis=1), preferred_element_type=F32)
        scores = prod[:, 0:width]
        for t in range(1, GROUP):
            scores = jnp.where(tok == t, prod[:, t * width:(t + 1) * width], scores)
        fresh = jnp.sum(q_f * kn_f, axis=-1, keepdims=True)
        here = lane == pos
        scores = jnp.where(here, fresh, scores) * scale
        scores = jnp.where(lane <= pos, scores, -1e30)
        top = jnp.max(scores, axis=-1, keepdims=True)
        expd = jnp.exp(scores - top)
        prob = (expd / jnp.sum(expd, axis=-1, keepdims=True)).astype(BF16).astype(F32)
        prob_new = jnp.sum(jnp.where(here, prob, 0.0), axis=-1, keepdims=True)
        prob_old = jnp.where(here, 0.0, prob).astype(BF16)
        ctx = lax.dot_general(prob_old, jnp.concatenate(vals, axis=0), (((1,), (1,)), ((), ())), preferred_element_type=F32)
        mixed = ctx[:, 0:width]
        for t in range(1, GROUP):
            mixed = jnp.where(tok == t, ctx[:, t * width:(t + 1) * width], mixed)
        mixed = mixed + prob_new * vn_f
        o_base = pl.multiple_of((step * per_step + g) * GROUP, GROUP)
        o_s[pl.ds(o_base, GROUP), :] = jnp.where(head_low, mixed[:GROUP], mixed[GROUP:])
        hot = jnp.concatenate([jnp.where((tok == t) & here, 1.0, 0.0).astype(BF16) for t in range(GROUP)], axis=1)
        k_col = lax.dot_general(kn_f.astype(BF16), hot, (((0,), (0,)), ((), ())), preferred_element_type=F32)
        v_col = lax.dot_general(vn_f.astype(BF16), hot, (((0,), (0,)), ((), ())), preferred_element_type=F32)
        for t in range(GROUP):
            p_t = pos_ref[(step * per_step + g) * GROUP + t]
            p_b = jnp.full((rows, width), p_t, jnp.int32).astype(F32).astype(BF16)
            mask = jnp.broadcast_to((lane_b == p_b)[None], (width // rows, rows, width))
            for ref, col, old in ((ko_ref, k_col, keys[t]), (vo_ref, v_col, vals[t])):
                new = col[:, t * width:(t + 1) * width].astype(BF16).reshape(width // rows, rows, width)
                ref[0, g * GROUP + t] = jnp.where(mask, new, old.reshape(width // rows, rows, width)).reshape(width, width)

    @pl.when(step == pl.num_programs(0) - 1)
    def _():
        part_ref[...] = jnp.dot(o_s[...].astype(BF16), wo_ref[layer], preferred_element_type=F32).astype(BF16)


def attention(layer, first, pos, x, gain, cos_tab, sin_tab, posb, wq, wk, wv, wo, kc, vc, prev):
    layers, tokens, width, cache_len = kc.shape
    model_dim = x.shape[1]
    head_dim = attention.head_dim
    whole = lambda a: pl.BlockSpec(a.shape, lambda i: (0,) * a.ndim)
    vmem = pl.BlockSpec(memory_space=pltpu.VMEM)
    cache = pl.BlockSpec((1, BLOCK, width, cache_len), lambda i: (layer, i, 0, 0))
    in_specs = [pl.BlockSpec(memory_space=pltpu.SMEM), whole(x), whole(gain), whole(cos_tab), whole(sin_tab), whole(posb),
                vmem, vmem, vmem, vmem, cache, cache]
    args = [pos, x, gain, cos_tab, sin_tab, posb, wq, wk, wv, wo, kc, vc]
    aliases = {}
    if not first:
        in_specs += [pl.BlockSpec(memory_space=pl.ANY)] * 2
        args += list(prev)
        aliases = {12: 1, 13: 2}
    return pl.pallas_call(
        functools.partial(attn_kernel, layer, head_dim, head_dim ** -0.5, first),
        grid=(tokens // BLOCK,),
        in_specs=in_specs,
        out_specs=[pl.BlockSpec((tokens, model_dim), lambda i: (0, 0)), cache, cache],
        out_shape=[jax.ShapeDtypeStruct((tokens, model_dim), BF16), jax.ShapeDtypeStruct(kc.shape, BF16), jax.ShapeDtypeStruct(vc.shape, BF16)],
        scratch_shapes=[pltpu.VMEM((2 * tokens, width), F32), pltpu.VMEM((2 * tokens, width), F32), pltpu.VMEM((2 * tokens, width), F32), pltpu.VMEM((tokens, width), F32)],
        input_output_aliases=aliases,
        compiler_params=pltpu.CompilerParams(dimension_semantics=("arbitrary",), vmem_limit_bytes=28 * 2 ** 20),
        name="attn",
    )(*args)


def mlp_kernel(n, layer, first, last, part_ref, x_ref, gm_ref, ga_ref, wg, wu, wd, h_ref, xo_ref,
               part2, rs_buf, ag_buf, rs_send, rs_recv, ag_send, ag_recv):
    data = lax.axis_index("data")
    me = lax.axis_index("model")
    blk = xo_ref.shape[0]
    peers = [lax.rem(me + d, n) for d in range(1, n)]
    barrier = pltpu.get_barrier_semaphore()
    for peer in peers:
        pl.semaphore_signal(barrier, inc=1, device_id=(data, peer), device_id_type=MESH)
    mine = pl.ds(pl.multiple_of(me * blk, blk), blk)
    order = sorted(range(1, n), key=lambda d: -min(d // 2, n // 2 - d // 2))

    def scatter(src, k):
        copies = []
        for d in order:
            rows = pl.ds(pl.multiple_of(peers[d - 1] * blk, blk), blk)
            copies.append(pltpu.make_async_remote_copy(
                src_ref=src.at[rows], dst_ref=rs_buf.at[k, d - 1], send_sem=rs_send.at[k, d - 1], recv_sem=rs_recv.at[k, d - 1],
                device_id=(data, peers[d - 1]), device_id_type=MESH))
            copies[-1].start()
        return copies

    def reduce(src, k, copies):
        total = src[mine, :].astype(F32)
        for copy in copies:
            copy.wait_recv()
        for d in range(1, n):
            total = total + rs_buf[k, d - 1].astype(F32)
        return total

    def gather(k, value):
        ag_buf[k, mine, :] = value
        copies = []
        for d in order:
            copies.append(pltpu.make_async_remote_copy(
                src_ref=ag_buf.at[k, mine], dst_ref=ag_buf.at[k, mine], send_sem=ag_send.at[k, d - 1], recv_sem=ag_recv.at[k, d - 1],
                device_id=(data, peers[d - 1]), device_id_type=MESH))
            copies[-1].start()
        return copies

    pl.semaphore_wait(barrier, n - 1)
    sent = scatter(part_ref, 0)
    x_old = (x_ref[mine, :] if first else x_ref[...]).astype(F32)
    x_mid = (x_old + reduce(part_ref, 0, sent)).astype(BF16)
    sent2 = gather(0, rms_rows(x_mid.astype(F32), gm_ref[...]))
    for copy in sent2:
        copy.wait_recv()
    hidden = ag_buf[0]
    nt = (((1,), (1,)), ((), ()))
    gate = lax.dot_general(hidden, wg[layer], nt, preferred_element_type=F32)
    up = lax.dot_general(hidden, wu[layer], nt, preferred_element_type=F32)
    act = (jax.nn.silu(gate) * up).astype(BF16)
    part2[...] = jnp.dot(act, wd[layer], preferred_element_type=F32).astype(BF16)
    sent3 = scatter(part2, 1)
    x_new = (x_mid.astype(F32) + reduce(part2, 1, sent3)).astype(BF16)
    xo_ref[...] = x_new
    sent4 = gather(1, x_new if last else rms_rows(x_new.astype(F32), ga_ref[...]))
    for copy in sent4:
        copy.wait_recv()
    h_ref[...] = ag_buf[1]
    for copies in (sent, sent2, sent3, sent4):
        for copy in copies:
            copy.wait_send()


def mlp(n, layer, layers, part, x, gm, ga, wg, wu, wd):
    tokens, model_dim = part.shape
    blk = tokens // n
    vmem = pl.BlockSpec(memory_space=pltpu.VMEM)
    return pl.pallas_call(
        functools.partial(mlp_kernel, n, layer, layer == 0, layer == layers - 1),
        in_specs=[vmem] * 7,
        out_specs=[vmem, vmem],
        out_shape=[jax.ShapeDtypeStruct((tokens, model_dim), BF16), jax.ShapeDtypeStruct((blk, model_dim), BF16)],
        scratch_shapes=[pltpu.VMEM((tokens, model_dim), BF16), pltpu.VMEM((2, n - 1, blk, model_dim), BF16), pltpu.VMEM((2, tokens, model_dim), BF16),
                        pltpu.SemaphoreType.DMA((2, n - 1)), pltpu.SemaphoreType.DMA((2, n - 1)),
                        pltpu.SemaphoreType.DMA((2, n - 1)), pltpu.SemaphoreType.DMA((2, n - 1))],
        compiler_params=pltpu.CompilerParams(collective_id=layer, has_side_effects=True, vmem_limit_bytes=20 * 2 ** 20),
        name="mlp",
    )(part, x, gm, ga, wg, wu, wd)


def solution(mesh):
    n = mesh.shape["model"]

    def local_step(hidden_in, positions, norm_attn, norm_mlp, w_query, w_key, w_value, w_out, w_gate, w_up, w_down, key_cache, value_cache):
        layers, tokens, cache_len, heads, head_dim = key_cache.shape
        attention.head_dim = head_dim
        width = heads * head_dim
        cos_tab, sin_tab = rope_tables(positions, head_dim, heads)
        posb = jnp.broadcast_to(positions.reshape(tokens // GROUP, 1, GROUP, 1), (tokens // GROUP, heads, GROUP, cache_len)).reshape(heads * tokens, cache_len)
        fold = lambda c: jnp.transpose(c, (0, 1, 3, 4, 2)).reshape(layers, tokens, width, cache_len)
        unfold = lambda c: jnp.transpose(c.reshape(layers, tokens, heads, head_dim, cache_len), (0, 1, 4, 2, 3))
        kc, vc = (pltpu.with_memory_space_constraint(fold(c), pltpu.HBM) for c in (key_cache, value_cache))
        wg, wu = jnp.swapaxes(w_gate, 1, 2), jnp.swapaxes(w_up, 1, 2)
        hidden, x_rows, prev = hidden_in, hidden_in, None
        for layer in range(layers):
            part, k_new, v_new = attention(layer, layer == 0, positions, hidden, norm_attn[layer:layer + 1], cos_tab, sin_tab, posb, w_query, w_key, w_value, w_out, kc, vc, prev)
            prev = (k_new, v_new)
            nxt = min(layer + 1, layers - 1)
            hidden, x_rows = mlp(n, layer, layers, part, x_rows, norm_mlp[layer:layer + 1], norm_attn[nxt:nxt + 1], wg, wu, w_down)
        return hidden, unfold(prev[0]), unfold(prev[1])

    row_spec = P("data", None)
    col_spec = P(None, None, "model")
    split_spec = P(None, "model", None)
    cache_spec = P(None, "data", None, "model", None)
    in_specs = (row_spec, P("data"), P(None, None), P(None, None), col_spec, col_spec, col_spec, split_spec, col_spec, col_spec, split_spec, cache_spec, cache_spec)
    out_specs = (row_spec, cache_spec, cache_spec)
    return jax.shard_map(local_step, mesh=mesh, in_specs=in_specs, out_specs=out_specs, check_vma=False)
```

time: 520 us -> 158 us (0.30)
  waiting for transfers between devices: 364 us -> 0 us
  Pallas kernels: 0 us -> 146 us
  matrix products: 70.8 us -> 0 us
  other arithmetic: 64.2 us -> 1.15 us
  between operations: 14.6 us -> 0.78 us
  local copies, waits for them, and re-layouts: 1.95 us -> 9.05 us
    psum x8 -> x0, waiting for transfers between devices: 363 us -> none  [the longest x4 182 us: local_step(): residual = add_residual(residual, lax.psum(attn_part, 'model'))]
    pallas_call x0 -> x8, Pallas kernels: none -> 146 us  [the longest x4 96.7 us: mlp(): pl.pallas_call(functools.partial(mlp_kernel, n, layer, layer == 0, layer...]
    dot_general x32 -> x0, matrix products: 70.8 us -> none  [the longest x4 18.4 us: attention(): jnp.einsum('bkgs,bskd->bkgd', attn_prob, v_cache, preferred_element_type=...]
    select_n x1 -> x0, other arithmetic: 23.5 us -> none  [attention(): v_cache = jnp.where(write_row, value_new[:, None], v_cache)]
    another operation x5 -> x0, other arithmetic: 23.3 us -> none  [the longest x1 23.2 us: local_step(): return (residual, jnp.stack(key_list), jnp.stack(value_list))]
    reduce_sum x8 -> x0, other arithmetic: 9.03 us -> none  [rms_norm(): jnp.mean(vals_f * vals_f, axis=-1, keepdims=True) + NORM_EPS]
    unnamed x14 -> x27, local copies, waits for them, and re-layouts: 0.04 us -> 7.23 us
  transfers between devices with their start and end apart: 8 -> 0, of which waited for: 8 -> 0; matrix products, arithmetic and copies ran while one was open for 9% -> 0% of each run, Pallas kernels for 0% -> 0%
where the time goes in v1:
time: 158 us; the launch traced here: 157 us
  Pallas kernels  146 us (92%)
  local copies, waits for them, and re-layouts  9.05 us (6%)
    pallas_call x4, Pallas kernels, mlp(): pl.pallas_call(functools.partial(mlp_kernel, n, layer, layer == 0, layer...  96.7 us
    pallas_call x4, Pallas kernels, attention(): pl.pallas_call(functools.partial(attn_kernel, layer, head_dim, head_dim *...  49.6 us
    unnamed x27, local copies, waits for them, and re-layouts  7.23 us

profile of v1, /device:TPU:113, one launch (start us, length us, event | category | flops | bytes accessed | tf_op | source)
XLA Modules:
  0.0 157.3 jit_solution(14478762426736304246)
XLA Ops:
  0.6 0.7 convert_element_type.3
  1.3 0.7 broadcast_in_dim.13
  2.1 0.1 broadcast_in_dim.15
  2.2 0.9 fusion.1
  3.0 0.1 broadcast_in_dim.16.refs_5_
  3.1 0.3 fusion
  3.5 0.2 pad_maximum_fusion
  3.6 0.0 copy-start.3
  3.6 1.2 copy-done.3
  4.9 0.0 copy-start.5
  4.9 1.2 copy-done.5
  6.1 0.0 copy-start.7
  6.1 1.2 copy-done.7
  7.3 0.0 copy-start.9
  7.3 1.2 copy-done.9
  8.5 0.0 copy-start.11
  8.5 0.9 copy-done.11
  9.5 0.0 copy-start.12
  9.5 0.7 copy-done.12
  10.1 0.0 copy-start
  10.2 0.0 copy-start.1
  10.2 0.0 copy-start.2
  10.2 0.0 copy-start.4
  10.2 0.0 copy-start.6
  10.2 0.0 copy-start.8
  10.2 0.0 copy-start.10
  10.2 13.0 %attn.4 = (bf16[128,1024]{1,0:T(8,128)(2,1)S(1)}, bf16[4,128,128,128]{3,2,1,0:T(8,128)(2,1)}, bf16[4,128,128,128]{3,2,1,0:T(8,128)(2,1)}) custom-call(s32[128]{0:T(128)S(1)} %copy-done.12, bf16[128,1024]{1,0:T(8,128)(2,1)S(1)} %copy-done.11, bf16[1,1024]{1,0:T(2,128)(2,1)S(1)} %get-tuple-element.55.refs_2_, f32[128,128]{1,0:T(8,128)S(1)} %get-tuple-element.52.refs_3_, ...), custom_call_target="tpu_custom_call" | custom-call | tf_op jit(solution)/shard_map/attn/pallas_call | solution.py:138
  23.2 0.0 copy-done
  23.2 0.0 copy-done.1
  23.2 0.0 copy-done.2
  23.2 25.8 %mlp.4 = (bf16[128,1024]{1,0:T(8,128)(2,1)S(1)}, bf16[16,1024]{1,0:T(8,128)(2,1)S(1)}) custom-call(bf16[128,1024]{1,0:T(8,128)(2,1)S(1)} %get-tuple-element.22.part_ref, bf16[128,1024]{1,0:T(8,128)(2,1)S(1)} %copy-done.11, bf16[1,1024]{1,0:T(2,128)(2,1)S(1)} %get-tuple-element.43.gm_ref, bf16[1,1024]{1,0:T(2,128)(2,1)S(1)} %get-tuple-element.56.ga_ref.refs_2_, ...), custom_call_target="tpu_custom_call" | custom-call | tf_op jit(solution)/shard_map/mlp/pallas_call | solution.py:220
  49.0 0.0 copy-done.4
  49.1 0.0 copy-done.6
  49.1 0.0 copy-done.8
  49.1 0.0 copy-done.10
  49.1 12.2 %attn.5 = (bf16[128,1024]{1,0:T(8,128)(2,1)S(1)}, bf16[4,128,128,128]{3,2,1,0:T(8,128)(2,1)}, bf16[4,128,128,128]{3,2,1,0:T(8,128)(2,1)}) custom-call(s32[128]{0:T(128)S(1)} %copy-done.12, bf16[128,1024]{1,0:T(8,128)(2,1)S(1)} %get-tuple-element.23.refs_1_, ...), custom_call_target="tpu_custom_call", output_to_operand_aliasing={{1}: (12, {}), {2}: (13, {})} | custom-call | tf_op jit(solution)/shard_map/attn/pallas_call | solution.py:138
  61.3 23.5 %mlp.5 = (bf16[128,1024]{1,0:T(8,128)(2,1)S(1)}, bf16[16,1024]{1,0:T(8,128)(2,1)S(1)}) custom-call(bf16[128,1024]{1,0:T(8,128)(2,1)S(1)} %get-tuple-element.26.part_ref, bf16[16,1024]{1,0:T(8,128)(2,1)S(1)} %get-tuple-element.27.x_ref, bf16[1,1024]{1,0:T(2,128)(2,1)S(1)} %get-tuple-element.42.gm_ref, bf16[1,1024]{1,0:T(2,128)(2,1)S(1)} %get-tuple-element.54.ga_ref.refs_2_, ...), custom_call_target="tpu_custom_call" | custom-call | tf_op jit(solution)/shard_map/mlp/pallas_call | solution.py:220
  84.8 12.2 %attn.6 = (bf16[128,1024]{1,0:T(8,128)(2,1)S(1)}, bf16[4,128,128,128]{3,2,1,0:T(8,128)(2,1)}, bf16[4,128,128,128]{3,2,1,0:T(8,128)(2,1)}) custom-call(s32[128]{0:T(128)S(1)} %copy-done.12, bf16[128,1024]{1,0:T(8,128)(2,1)S(1)} %get-tuple-element.28.refs_1_, ...), custom_call_target="tpu_custom_call", output_to_operand_aliasing={{1}: (12, {}), {2}: (13, {})} | custom-call | tf_op jit(solution)/shard_map/attn/pallas_call | solution.py:138
  97.0 23.2 %mlp.6 = (bf16[128,1024]{1,0:T(8,128)(2,1)S(1)}, bf16[16,1024]{1,0:T(8,128)(2,1)S(1)}) custom-call(bf16[128,1024]{1,0:T(8,128)(2,1)S(1)} %get-tuple-element.31.part_ref, bf16[16,1024]{1,0:T(8,128)(2,1)S(1)} %get-tuple-element.32.x_ref, bf16[1,1024]{1,0:T(2,128)(2,1)S(1)} %get-tuple-element.44.gm_ref, bf16[1,1024]{1,0:T(2,128)(2,1)S(1)} %get-tuple-element.57.ga_ref.refs_2_, ...), custom_call_target="tpu_custom_call" | custom-call | tf_op jit(solution)/shard_map/mlp/pallas_call | solution.py:220
  120.3 12.2 %attn.7 = (bf16[128,1024]{1,0:T(8,128)(2,1)S(1)}, bf16[4,128,128,128]{3,2,1,0:T(8,128)(2,1)}, bf16[4,128,128,128]{3,2,1,0:T(8,128)(2,1)}) custom-call(s32[128]{0:T(128)S(1)} %copy-done.12, bf16[128,1024]{1,0:T(8,128)(2,1)S(1)} %get-tuple-element.33.refs_1_, ...), custom_call_target="tpu_custom_call", output_to_operand_aliasing={{1}: (12, {}), {2}: (13, {})} | custom-call | tf_op jit(solution)/shard_map/attn/pallas_call | solution.py:138
  132.4 24.1 %mlp.7 = (bf16[128,1024]{1,0:T(8,128)(2,1)S(1)}, bf16[16,1024]{1,0:T(8,128)(2,1)}) custom-call(bf16[128,1024]{1,0:T(8,128)(2,1)S(1)} %get-tuple-element.36.part_ref, bf16[16,1024]{1,0:T(8,128)(2,1)S(1)} %get-tuple-element.37.x_ref, bf16[1,1024]{1,0:T(2,128)(2,1)S(1)} %get-tuple-element.41.gm_ref, bf16[1,1024]{1,0:T(2,128)(2,1)S(1)} %get-tuple-element.57.ga_ref.refs_2_, ...), custom_call_target="tpu_custom_call" | custom-call | tf_op jit(solution)/shard_map/mlp/pallas_call | solution.py:220
  156.6 0.7 copy.30
  (2 shorter events, 0.0 us)
Async XLA Ops:
  3.6 1.2 copy-start.3
  4.9 1.2 copy-start.5
  6.1 1.2 copy-start.7
  7.3 1.2 copy-start.9
  8.5 0.9 copy-start.11
  9.5 0.7 copy-start.12
  10.1 13.1 %copy-start = (bf16[4,1024,352]{1,2,0:T(8,128)(2,1)S(1)}, bf16[4,1024,352]{1,2,0:T(8,128)(2,1)}, u32[]{:S(2)}) copy-start(bf16[4,1024,352]{1,2,0:T(8,128)(2,1)} %param.21) | copy-start | bytes 8650756
  10.2 13.1 %copy-start.1 = (bf16[4,1024,352]{1,2,0:T(8,128)(2,1)S(1)}, bf16[4,1024,352]{1,2,0:T(8,128)(2,1)}, u32[]{:S(2)}) copy-start(bf16[4,1024,352]{1,2,0:T(8,128)(2,1)} %param.22) | copy-start | bytes 8650756
  10.2 13.1 %copy-start.2 = (bf16[4,352,1024]{2,1,0:T(8,128)(2,1)S(1)}, bf16[4,352,1024]{2,1,0:T(8,128)(2,1)}, u32[]{:S(2)}) copy-start(bf16[4,352,1024]{2,1,0:T(8,128)(2,1)} %wd.7) | copy-start | bytes 8650756
  10.2 38.9 %copy-start.4 = (bf16[4,1024,128]{2,1,0:T(8,128)(2,1)S(1)}, bf16[4,1024,128]{2,1,0:T(8,128)(2,1)}, u32[]{:S(2)}) copy-start(bf16[4,1024,128]{2,1,0:T(8,128)(2,1)} %refs_6_.7) | copy-start | bytes 3145732
  10.2 38.9 %copy-start.6 = (bf16[4,1024,128]{2,1,0:T(8,128)(2,1)S(1)}, bf16[4,1024,128]{2,1,0:T(8,128)(2,1)}, u32[]{:S(2)}) copy-start(bf16[4,1024,128]{2,1,0:T(8,128)(2,1)} %refs_7_.7) | copy-start | bytes 3145732
  10.2 38.9 %copy-start.8 = (bf16[4,1024,128]{2,1,0:T(8,128)(2,1)S(1)}, bf16[4,1024,128]{2,1,0:T(8,128)(2,1)}, u32[]{:S(2)}) copy-start(bf16[4,1024,128]{2,1,0:T(8,128)(2,1)} %refs_8_.7) | copy-start | bytes 3145732
  10.2 38.9 %copy-start.10 = (bf16[4,128,1024]{2,1,0:T(8,128)(2,1)S(1)}, bf16[4,128,1024]{2,1,0:T(8,128)(2,1)}, u32[]{:S(2)}) copy-start(bf16[4,128,1024]{2,1,0:T(8,128)(2,1)} %refs_9_.7) | copy-start | bytes 3145732

commit v2 on v1

v2 whole, which is shorter than its diff:
```python
import functools
import numpy as np
import jax
import jax.numpy as jnp
from jax import lax
from jax.experimental import pallas as pl
from jax.experimental.pallas import tpu as pltpu
from jax.sharding import PartitionSpec as P

NORM_EPS = 1e-6
ROPE_BASE = 10000.0
MESH = pl.DeviceIdType.MESH
GROUP = 8
BLOCK = 32
F32 = jnp.float32
BF16 = jnp.bfloat16


def rms_rows(vals_f, gain):
    inv_rms = lax.rsqrt(jnp.mean(vals_f * vals_f, axis=-1, keepdims=True) + NORM_EPS)
    return (vals_f * inv_rms * gain.astype(F32)).astype(BF16)


def rope_freqs(head_dim, heads):
    half = head_dim // 2
    inv_freq = ROPE_BASE ** (-np.arange(half, dtype=np.float32) / np.float32(half))
    return np.tile(inv_freq.astype(np.float32), 2 * heads)[None, :]


def attn_kernel(layer, head_dim, scale, first, *refs):
    if first:
        (pos_ref, freq_ref, x_ref, gain_ref, wq_ref, wk_ref, wv_ref, wo_ref, k_ref, v_ref,
         part_ref, ko_ref, vo_ref, cos_ref, sin_ref, posr_ref, q_s, kn_s, vn_s, o_s) = refs
    else:
        (cos_ref, sin_ref, posr_ref, x_ref, wq_ref, wk_ref, wv_ref, wo_ref, k_ref, v_ref, _, _,
         part_ref, ko_ref, vo_ref, q_s, kn_s, vn_s, o_s) = refs
    step = pl.program_id(0)
    tokens, width = q_s.shape[0] // 2, q_s.shape[1]
    half = head_dim // 2
    groups = tokens // GROUP

    def by_head(vals):
        lane = lax.broadcasted_iota(jnp.int32, (groups, GROUP, width), 2)
        vals3 = vals.reshape(groups, GROUP, width)
        low = jnp.where(lane < head_dim, vals3, 0.0)
        high = jnp.where(lane < head_dim, 0.0, vals3)
        return jnp.concatenate([low, high], axis=1).reshape(2 * tokens, width)

    @pl.when(step == 0)
    def _():
        lane = lax.broadcasted_iota(jnp.int32, (tokens, width), 1)
        lower = lax.rem(lane, head_dim) < half
        if first:
            posr = jnp.transpose(jnp.broadcast_to(pos_ref[...].astype(F32), (width, tokens)))
            posr_ref[...] = posr
            angle = posr * freq_ref[...]
            cos_ref[...] = jnp.cos(angle)
            sin_ref[...] = jnp.where(lower, -1.0, 1.0) * jnp.sin(angle)
            hidden = rms_rows(x_ref[...].astype(F32), gain_ref[layer:layer + 1, :])
        else:
            hidden = x_ref[...]

        def rope(vals):
            turned = jnp.where(lower, pltpu.roll(vals, width - half, 1), pltpu.roll(vals, half, 1))
            return (vals * cos_ref[...] + turned * sin_ref[...]).astype(BF16).astype(F32)

        def project(w_ref):
            return jnp.dot(hidden, w_ref[0 if first else layer], preferred_element_type=F32).astype(BF16).astype(F32)

        q_s[...] = by_head(rope(project(wq_ref)))
        kn_s[...] = by_head(rope(project(wk_ref)))
        vn_s[...] = by_head(project(wv_ref))

    rows = 2 * GROUP
    row = lax.broadcasted_iota(jnp.int32, (rows, width), 0)
    tok = lax.rem(row, GROUP)
    lane = lax.broadcasted_iota(jnp.int32, (rows, width), 1).astype(F32)
    lane_b = lane.astype(BF16)
    head_low = lax.broadcasted_iota(jnp.int32, (GROUP, width), 1) < head_dim
    per_step = BLOCK // GROUP
    for g in range(per_step):
        base = pl.multiple_of((step * per_step + g) * rows, rows)
        tok_base = pl.multiple_of((step * per_step + g) * GROUP, GROUP)
        q_f = q_s[pl.ds(base, rows), :]
        kn_f = kn_s[pl.ds(base, rows), :]
        vn_f = vn_s[pl.ds(base, rows), :]
        pos8 = posr_ref[pl.ds(tok_base, GROUP), :]
        pos = jnp.concatenate([pos8, pos8], axis=0)
        if first:
            keys = [k_ref[0, g * GROUP + t] for t in range(GROUP)]
            vals = [v_ref[0, g * GROUP + t] for t in range(GROUP)]
        else:
            keys = [k_ref[tok_base + t] for t in range(GROUP)]
            vals = [v_ref[tok_base + t] for t in range(GROUP)]
        prod = jnp.dot(q_f.astype(BF16), jnp.concatenate(keys, axis=1), preferred_element_type=F32)
        scores = prod[:, 0:width]
        for t in range(1, GROUP):
            scores = jnp.where(tok == t, prod[:, t * width:(t + 1) * width], scores)
        fresh = jnp.sum(q_f * kn_f, axis=-1, keepdims=True)
        here = lane == pos
        scores = jnp.where(here, fresh, scores) * scale
        scores = jnp.where(lane <= pos, scores, -1e30)
        top = jnp.max(scores, axis=-1, keepdims=True)
        expd = jnp.exp(scores - top)
        prob = (expd / jnp.sum(expd, axis=-1, keepdims=True)).astype(BF16).astype(F32)
        prob_new = jnp.sum(jnp.where(here, prob, 0.0), axis=-1, keepdims=True)
        prob_old = jnp.where(here, 0.0, prob).astype(BF16)
        ctx = lax.dot_general(prob_old, jnp.concatenate(vals, axis=0), (((1,), (1,)), ((), ())), preferred_element_type=F32)
        mixed = ctx[:, 0:width]
        for t in range(1, GROUP):
            mixed = jnp.where(tok == t, ctx[:, t * width:(t + 1) * width], mixed)
        mixed = mixed + prob_new * vn_f
        o_s[pl.ds(tok_base, GROUP), :] = jnp.where(head_low, mixed[:GROUP], mixed[GROUP:])
        hot = jnp.concatenate([jnp.where((tok == t) & here, 1.0, 0.0).astype(BF16) for t in range(GROUP)], axis=1)
        k_col = lax.dot_general(kn_f.astype(BF16), hot, (((0,), (0,)), ((), ())), preferred_element_type=F32)
        v_col = lax.dot_general(vn_f.astype(BF16), hot, (((0,), (0,)), ((), ())), preferred_element_type=F32)
        for t in range(GROUP):
            p_b = jnp.broadcast_to(posr_ref[pl.ds(tok_base + t, 1), :], (rows, width)).astype(BF16)
            mask = jnp.broadcast_to((lane_b == p_b)[None], (width // rows, rows, width))
            for ref, col, old in ((ko_ref, k_col, keys[t]), (vo_ref, v_col, vals[t])):
                new = col[:, t * width:(t + 1) * width].astype(BF16).reshape(width // rows, rows, width)
                ref[0, g * GROUP + t] = jnp.where(mask, new, old.reshape(width // rows, rows, width)).reshape(width, width)

    @pl.when(step == pl.num_programs(0) - 1)
    def _():
        part_ref[...] = jnp.dot(o_s[...].astype(BF16), wo_ref[0 if first else layer], preferred_element_type=F32).astype(BF16)


def attention(layer, head_dim, lead, x, weights, caches, shape, prev):
    first = layer == 0
    layers, tokens, width, cache_len = shape
    model_dim = x.shape[1]
    vmem = pl.BlockSpec(memory_space=pltpu.VMEM)
    whole = lambda a: pl.BlockSpec(a.shape, lambda i: (0,) * a.ndim)
    of_layer = lambda a: pl.BlockSpec((1,) + a.shape[1:], lambda i: (layer,) + (0,) * (a.ndim - 1))
    cache = pl.BlockSpec((1, BLOCK, width, cache_len), lambda i: (layer, i, 0, 0))
    table = jax.ShapeDtypeStruct((tokens, width), F32)
    out_specs = [pl.BlockSpec((tokens, model_dim), lambda i: (0, 0)), cache, cache]
    out_shape = [jax.ShapeDtypeStruct((tokens, model_dim), BF16), jax.ShapeDtypeStruct(shape, BF16), jax.ShapeDtypeStruct(shape, BF16)]
    aliases = {}
    if first:
        pos, freq, gain = lead
        in_specs = [whole(pos), whole(freq), whole(x), whole(gain)] + [of_layer(w) for w in weights] + [cache, cache]
        args = [pos, freq, x, gain, *weights, *caches]
        out_specs += [pl.BlockSpec((tokens, width), lambda i: (0, 0))] * 3
        out_shape += [table] * 3
    else:
        in_specs = [vmem] * 10 + [pl.BlockSpec(memory_space=pl.ANY)] * 2
        args = [*lead, x, *weights, *caches, *prev]
        aliases = {10: 1, 11: 2}
    return pl.pallas_call(
        functools.partial(attn_kernel, layer, head_dim, head_dim ** -0.5, first),
        grid=(tokens // BLOCK,),
        in_specs=in_specs,
        out_specs=out_specs,
        out_shape=out_shape,
        scratch_shapes=[pltpu.VMEM((2 * tokens, width), F32), pltpu.VMEM((2 * tokens, width), F32), pltpu.VMEM((2 * tokens, width), F32), pltpu.VMEM((tokens, width), F32)],
        input_output_aliases=aliases,
        compiler_params=pltpu.CompilerParams(dimension_semantics=("arbitrary",), vmem_limit_bytes=28 * 2 ** 20),
        name="attn",
    )(*args)


def mlp_kernel(n, layer, first, last, *refs):
    if last:
        part_ref, x_ref, gm_ref, ga_ref, wg, wu, wd, h_ref, xo_ref, part2, rs_buf, ag_buf, rs_send, rs_recv, ag_send, ag_recv = refs
        loads = []
    else:
        (part_ref, x_ref, gm_ref, ga_ref, wg, wu, wd, kc_ref, vc_ref, h_ref, xo_ref, k_out, v_out,
         part2, rs_buf, ag_buf, rs_send, rs_recv, ag_send, ag_recv, load_sem) = refs
        loads = [pltpu.make_async_copy(src.at[layer + 1], dst, load_sem.at[i]) for i, (src, dst) in enumerate(((kc_ref, k_out), (vc_ref, v_out)))]
    data = lax.axis_index("data")
    me = lax.axis_index("model")
    blk = xo_ref.shape[0]
    peers = [lax.rem(me + d, n) for d in range(1, n)]
    barrier = pltpu.get_barrier_semaphore()
    for peer in peers:
        pl.semaphore_signal(barrier, inc=1, device_id=(data, peer), device_id_type=MESH)
    mine = pl.ds(pl.multiple_of(me * blk, blk), blk)
    order = sorted(range(1, n), key=lambda d: -min(d // 2, n // 2 - d // 2))

    def scatter(src, k):
        copies = []
        for d in order:
            rows = pl.ds(pl.multiple_of(peers[d - 1] * blk, blk), blk)
            copies.append(pltpu.make_async_remote_copy(
                src_ref=src.at[rows], dst_ref=rs_buf.at[k, d - 1], send_sem=rs_send.at[k, d - 1], recv_sem=rs_recv.at[k, d - 1],
                device_id=(data, peers[d - 1]), device_id_type=MESH))
            copies[-1].start()
        return copies

    def reduce(src, k, copies):
        total = src[mine, :].astype(F32)
        for copy in copies:
            copy.wait_recv()
        for d in range(1, n):
            total = total + rs_buf[k, d - 1].astype(F32)
        return total

    def gather(k, value):
        ag_buf[k, mine, :] = value
        copies = []
        for d in order:
            copies.append(pltpu.make_async_remote_copy(
                src_ref=ag_buf.at[k, mine], dst_ref=ag_buf.at[k, mine], send_sem=ag_send.at[k, d - 1], recv_sem=ag_recv.at[k, d - 1],
                device_id=(data, peers[d - 1]), device_id_type=MESH))
            copies[-1].start()
        return copies

    for load in loads:
        load.start()
    pl.semaphore_wait(barrier, n - 1)
    sent = scatter(part_ref, 0)
    x_old = (x_ref[mine, :] if first else x_ref[...]).astype(F32)
    x_mid = (x_old + reduce(part_ref, 0, sent)).astype(BF16)
    sent2 = gather(0, rms_rows(x_mid.astype(F32), gm_ref[layer:layer + 1, :]))
    for copy in sent2:
        copy.wait_recv()
    hidden = ag_buf[0]
    nt = (((1,), (1,)), ((), ()))
    gate = lax.dot_general(hidden, wg[layer], nt, preferred_element_type=F32)
    up = lax.dot_general(hidden, wu[layer], nt, preferred_element_type=F32)
    act = (jax.nn.silu(gate) * up).astype(BF16)
    part2[...] = jnp.dot(act, wd[layer], preferred_element_type=F32).astype(BF16)
    sent3 = scatter(part2, 1)
    x_new = (x_mid.astype(F32) + reduce(part2, 1, sent3)).astype(BF16)
    xo_ref[...] = x_new
    sent4 = gather(1, x_new if last else rms_rows(x_new.astype(F32), ga_ref[layer + 1:layer + 2, :]))
    for copy in sent4:
        copy.wait_recv()
    h_ref[...] = ag_buf[1]
    for copies in (sent, sent2, sent3, sent4):
        for copy in copies:
            copy.wait_send()
    for load in loads:
        load.wait()


def mlp(n, layer, part, x, gm, ga, wg, wu, wd, kc, vc):
    tokens, model_dim = part.shape
    blk = tokens // n
    last = layer == kc.shape[0] - 1
    vmem = pl.BlockSpec(memory_space=pltpu.VMEM)
    ahead = [] if last else [kc, vc]
    return pl.pallas_call(
        functools.partial(mlp_kernel, n, layer, layer == 0, last),
        in_specs=[vmem] * 7 + [pl.BlockSpec(memory_space=pl.ANY)] * len(ahead),
        out_specs=[vmem] * (2 + len(ahead)),
        out_shape=[jax.ShapeDtypeStruct((tokens, model_dim), BF16), jax.ShapeDtypeStruct((blk, model_dim), BF16)] + [pltpu.VMEM(c.shape[1:], BF16) for c in ahead],
        scratch_shapes=[pltpu.VMEM((tokens, model_dim), BF16), pltpu.VMEM((2, n - 1, blk, model_dim), BF16), pltpu.VMEM((2, tokens, model_dim), BF16),
                        pltpu.SemaphoreType.DMA((2, n - 1)), pltpu.SemaphoreType.DMA((2, n - 1)),
                        pltpu.SemaphoreType.DMA((2, n - 1)), pltpu.SemaphoreType.DMA((2, n - 1))] + ([] if last else [pltpu.SemaphoreType.DMA((2,))]),
        compiler_params=pltpu.CompilerParams(collective_id=layer, has_side_effects=True, vmem_limit_bytes=20 * 2 ** 20),
        name="mlp",
    )(part, x, gm, ga, wg, wu, wd, *ahead)


def solution(mesh):
    n = mesh.shape["model"]

    def local_step(hidden_in, positions, norm_attn, norm_mlp, w_query, w_key, w_value, w_out, w_gate, w_up, w_down, key_cache, value_cache):
        layers, tokens, cache_len, heads, head_dim = key_cache.shape
        shape = (layers, tokens, heads * head_dim, cache_len)
        in_hbm = lambda a: pltpu.with_memory_space_constraint(a, pltpu.HBM)
        unfold = lambda c: jnp.transpose(c.reshape(layers, tokens, heads, head_dim, cache_len), (0, 1, 4, 2, 3))
        kc, vc = (in_hbm(jnp.transpose(c, (0, 1, 3, 4, 2)).reshape(shape)) for c in (key_cache, value_cache))
        wg, wu = jnp.swapaxes(w_gate, 1, 2), jnp.swapaxes(w_up, 1, 2)
        weights = (w_query, w_key, w_value, w_out)
        freq = jnp.asarray(rope_freqs(head_dim, heads))
        part, k_new, v_new, *tables = attention(0, head_dim, (in_hbm(positions.reshape(1, tokens)), freq, in_hbm(norm_attn)), in_hbm(hidden_in), [in_hbm(w) for w in weights], (kc, vc), shape, None)
        x_rows = hidden_in
        for layer in range(layers):
            hidden, x_rows, *caches = mlp(n, layer, part, x_rows, norm_mlp, norm_attn, wg, wu, w_down, kc, vc)
            if layer + 1 < layers:
                part, k_new, v_new = attention(layer + 1, head_dim, tables, hidden, weights, caches, shape, (k_new, v_new))
        return hidden, unfold(k_new), unfold(v_new)

    row_spec = P("data", None)
    col_spec = P(None, None, "model")
    split_spec = P(None, "model", None)
    cache_spec = P(None, "data", None, "model", None)
    in_specs = (row_spec, P("data"), P(None, None), P(None, None), col_spec, col_spec, col_spec, split_spec, col_spec, col_spec, split_spec, cache_spec, cache_spec)
    out_specs = (row_spec, cache_spec, cache_spec)
    return jax.shard_map(local_step, mesh=mesh, in_specs=in_specs, out_specs=out_specs, check_vma=False)
```

time: 158 us -> 143 us (0.905)
  local copies, waits for them, and re-layouts: 9.05 us -> 1.4 us
  Pallas kernels: 146 us -> 141 us
    unnamed x27 -> x23, local copies, waits for them, and re-layouts: 7.23 us -> 1.4 us
    pallas_call x4, Pallas kernels: 49.6 us -> 44.1 us  [attention(): pl.pallas_call(functools.partial(attn_kernel, layer, head_dim, head_dim *...]
where the time goes in v2:
time: 143 us
  Pallas kernels  141 us (99%)
    pallas_call x4, Pallas kernels, mlp(): pl.pallas_call(functools.partial(mlp_kernel, n, layer, layer == 0, last),...  96.9 us
    pallas_call x4, Pallas kernels, attention(): pl.pallas_call(functools.partial(attn_kernel, layer, head_dim, head_dim *...  44.1 us

profile of v2, /device:TPU:113, one launch (start us, length us, event | category | flops | bytes accessed | tf_op | source)
XLA Modules:
  0.0 143.2 jit_solution(116929430412936538)
XLA Ops:
  0.6 0.0 copy-start.10
  0.6 0.6 copy-done.10
  1.3 0.0 copy-start
  1.3 0.0 copy-start.1
  1.3 0.0 copy-start.2
  1.3 0.0 copy-start.7
  1.3 0.0 copy-start.8
  1.3 0.0 copy-start.9
  1.3 12.9 %attn.4 = (bf16[128,1024]{1,0:T(8,128)(2,1)S(1)}, bf16[4,128,128,128]{3,2,1,0:T(8,128)(2,1)}, bf16[4,128,128,128]{3,2,1,0:T(8,128)(2,1)}, f32[128,128]{1,0:T(8,1...) custom-call(s32[1,128]{1,0:T(1,128)} %bitcast.33, f32[1,128]{1,0:T(1,128)S(1)} %copy-done.10, ...), custom_call_target="tpu_custom_call" | custom-call | tf_op jit(solution)/shard_map/attn/pallas_call | solution.py:151
  14.3 0.0 copy-done
  14.3 0.0 copy-done.1
  14.3 0.0 copy-done.2
  14.3 0.0 copy-done.7
  14.3 0.0 copy-done.8
  14.3 0.0 copy-done.9
  14.3 0.0 copy-start.3
  14.3 0.0 copy-start.4
  14.3 0.0 copy-start.5
  14.4 0.0 copy-start.6
  14.4 25.8 %mlp.4 = (bf16[128,1024]{1,0:T(8,128)(2,1)S(1)}, bf16[16,1024]{1,0:T(8,128)(2,1)S(1)}, bf16[128,128,128]{2,1,0:T(8,128)(2,1)S(1)}, bf16[128,128,128]{2,1,0:T(8,128)(2,1)S(1)}) custom-call(bf16[128,1024]{1,0:T(8,128)(2,1)S(1)} %get-tuple-element.34.refs_0_, bf16[128,1024]{1,0:T(8,128)(2,1)S(1)} %copy-done.7, bf16[4,1024]{1,0:T(4,128)(2,1)S(1)} %copy-done.9, ...), custom_call_target="tpu_custom_call" | custom-call | tf_op jit(solution)/shard_map/mlp/pallas_call | solution.py:245
  40.2 0.0 copy-done.3
  40.2 0.0 copy-done.4
  40.2 0.0 copy-done.5
  40.2 0.0 copy-done.6
  40.2 10.4 %attn.5 = (bf16[128,1024]{1,0:T(8,128)(2,1)S(1)}, bf16[4,128,128,128]{3,2,1,0:T(8,128)(2,1)}, bf16[4,128,128,128]{3,2,1,0:T(8,128)(2,1)}) custom-call(f32[128,128]{1,0:T(8,128)S(1)} %get-tuple-element.31.refs_0_, f32[128,128]{1,0:T(8,128)S(1)} %get-tuple-element.32.refs_1_, ...), custom_call_target="tpu_custom_call", output_to_operand_aliasing={{1}: (10, {}), {2}: (11, {})} | custom-call | tf_op jit(solution)/shard_map/attn/pallas_call | solution.py:151
  50.6 23.6 %mlp.5 = (bf16[128,1024]{1,0:T(8,128)(2,1)S(1)}, bf16[16,1024]{1,0:T(8,128)(2,1)S(1)}, bf16[128,128,128]{2,1,0:T(8,128)(2,1)S(1)}, bf16[128,128,128]{2,1,0:T(8,128)(2,1)S(1)}) custom-call(bf16[128,1024]{1,0:T(8,128)(2,1)S(1)} %get-tuple-element.40.refs_0_, bf16[16,1024]{1,0:T(8,128)(2,1)S(1)} %get-tuple-element.41.refs_1_, bf16[4,1024]{1,0:T(4,128)(2,1)S(1)} %copy-done.9, ...), custom_call_target="tpu_custom_call" | custom-call | tf_op jit(solution)/shard_map/mlp/pallas_call | solution.py:245
  74.2 10.4 %attn.6 = (bf16[128,1024]{1,0:T(8,128)(2,1)S(1)}, bf16[4,128,128,128]{3,2,1,0:T(8,128)(2,1)}, bf16[4,128,128,128]{3,2,1,0:T(8,128)(2,1)}) custom-call(f32[128,128]{1,0:T(8,128)S(1)} %get-tuple-element.31.refs_0_, f32[128,128]{1,0:T(8,128)S(1)} %get-tuple-element.32.refs_1_, ...), custom_call_target="tpu_custom_call", output_to_operand_aliasing={{1}: (10, {}), {2}: (11, {})} | custom-call | tf_op jit(solution)/shard_map/attn/pallas_call | solution.py:151
  84.6 23.3 %mlp.6 = (bf16[128,1024]{1,0:T(8,128)(2,1)S(1)}, bf16[16,1024]{1,0:T(8,128)(2,1)S(1)}, bf16[128,128,128]{2,1,0:T(8,128)(2,1)S(1)}, bf16[128,128,128]{2,1,0:T(8,128)(2,1)S(1)}) custom-call(bf16[128,1024]{1,0:T(8,128)(2,1)S(1)} %get-tuple-element.47.refs_0_, bf16[16,1024]{1,0:T(8,128)(2,1)S(1)} %get-tuple-element.48.refs_1_, bf16[4,1024]{1,0:T(4,128)(2,1)S(1)} %copy-done.9, ...), custom_call_target="tpu_custom_call" | custom-call | tf_op jit(solution)/shard_map/mlp/pallas_call | solution.py:245
  107.9 10.4 %attn.7 = (bf16[128,1024]{1,0:T(8,128)(2,1)S(1)}, bf16[4,128,128,128]{3,2,1,0:T(8,128)(2,1)}, bf16[4,128,128,128]{3,2,1,0:T(8,128)(2,1)}) custom-call(f32[128,128]{1,0:T(8,128)S(1)} %get-tuple-element.31.refs_0_, f32[128,128]{1,0:T(8,128)S(1)} %get-tuple-element.32.refs_1_, ...), custom_call_target="tpu_custom_call", output_to_operand_aliasing={{1}: (10, {}), {2}: (11, {})} | custom-call | tf_op jit(solution)/shard_map/attn/pallas_call | solution.py:151
  118.3 24.2 %mlp.7 = (bf16[128,1024]{1,0:T(8,128)(2,1)S(1)}, bf16[16,1024]{1,0:T(8,128)(2,1)}) custom-call(bf16[128,1024]{1,0:T(8,128)(2,1)S(1)} %get-tuple-element.54.refs_0_, bf16[16,1024]{1,0:T(8,128)(2,1)S(1)} %get-tuple-element.55.refs_1_, bf16[4,1024]{1,0:T(4,128)(2,1)S(1)} %copy-done.9, bf16[4,1024]{1,0:T(4,128)(2,1)S(1)} %copy-done.8, ...), custom_call_target="tpu_custom_call" | custom-call | tf_op jit(solution)/shard_map/mlp/pallas_call | solution.py:245
  142.5 0.7 copy.30
Async XLA Ops:
  0.6 0.7 copy-start.10
  1.3 13.0 %copy-start = (bf16[4,1024,352]{1,2,0:T(8,128)(2,1)S(1)}, bf16[4,1024,352]{1,2,0:T(8,128)(2,1)}, u32[]{:S(2)}) copy-start(bf16[4,1024,352]{1,2,0:T(8,128)(2,1)} %param.22) | copy-start | bytes 8650756
  1.3 13.0 %copy-start.1 = (bf16[4,1024,352]{1,2,0:T(8,128)(2,1)S(1)}, bf16[4,1024,352]{1,2,0:T(8,128)(2,1)}, u32[]{:S(2)}) copy-start(bf16[4,1024,352]{1,2,0:T(8,128)(2,1)} %param.23) | copy-start | bytes 8650756
  1.3 13.0 %copy-start.2 = (bf16[4,352,1024]{2,1,0:T(8,128)(2,1)S(1)}, bf16[4,352,1024]{2,1,0:T(8,128)(2,1)}, u32[]{:S(2)}) copy-start(bf16[4,352,1024]{2,1,0:T(8,128)(2,1)} %refs_6_.15) | copy-start | bytes 8650756
  1.3 13.0 %copy-start.7 = (bf16[128,1024]{1,0:T(8,128)(2,1)S(1)}, bf16[128,1024]{1,0:T(8,128)(2,1)}, u32[]{:S(2)}) copy-start(bf16[128,1024]{1,0:T(8,128)(2,1)} %refs_1_.2) | copy-start | bytes 786436
  1.3 13.0 %copy-start.8 = (bf16[4,1024]{1,0:T(4,128)(2,1)S(1)}, bf16[4,1024]{1,0:T(4,128)(2,1)}, u32[]{:S(2)}) copy-start(bf16[4,1024]{1,0:T(4,128)(2,1)} %refs_3_.9) | copy-start | bytes 24580
  1.3 13.0 %copy-start.9 = (bf16[4,1024]{1,0:T(4,128)(2,1)S(1)}, bf16[4,1024]{1,0:T(4,128)(2,1)}, u32[]{:S(2)}) copy-start(bf16[4,1024]{1,0:T(4,128)(2,1)} %refs_2_.9) | copy-start | bytes 24580
  14.3 25.9 %copy-start.3 = (bf16[4,1024,128]{2,1,0:T(8,128)(2,1)S(1)}, bf16[4,1024,128]{2,1,0:T(8,128)(2,1)}, u32[]{:S(2)}) copy-start(bf16[4,1024,128]{2,1,0:T(8,128)(2,1)} %refs_4_.7) | copy-start | bytes 3145732
  14.3 25.9 %copy-start.4 = (bf16[4,1024,128]{2,1,0:T(8,128)(2,1)S(1)}, bf16[4,1024,128]{2,1,0:T(8,128)(2,1)}, u32[]{:S(2)}) copy-start(bf16[4,1024,128]{2,1,0:T(8,128)(2,1)} %refs_5_.7) | copy-start | bytes 3145732
  14.3 25.9 %copy-start.5 = (bf16[4,1024,128]{2,1,0:T(8,128)(2,1)S(1)}, bf16[4,1024,128]{2,1,0:T(8,128)(2,1)}, u32[]{:S(2)}) copy-start(bf16[4,1024,128]{2,1,0:T(8,128)(2,1)} %refs_6_.14) | copy-start | bytes 3145732
  14.4 25.9 %copy-start.6 = (bf16[4,128,1024]{2,1,0:T(8,128)(2,1)S(1)}, bf16[4,128,1024]{2,1,0:T(8,128)(2,1)}, u32[]{:S(2)}) copy-start(bf16[4,128,1024]{2,1,0:T(8,128)(2,1)} %refs_7_.7) | copy-start | bytes 3145732
